TPU v7x, 32 devices: a whole 2x2x4 slice. The times are simulated.
32 devices in a mesh: genes: 16 (over z, y, core), cols: 2 (over x).
Axes of the slice: x: 2, y: 2, z: 4, core: 2. Of those that a mesh axis runs over, the one named last changes fastest.
Arguments:
- expression: float32 [384, 40960], P(None, ('genes', 'cols')), may hold values from -200 to 200
- resample: int32 [384], replicated, may hold values from 0 to 383
- labels: int32 [40960, 300], P(('genes', 'cols')), may hold values from 0 to 1, as said below
- ref_kim: float32 [40960], P(('genes', 'cols')), may hold values from 0 to 1
Outputs:
- connectivity: float32 [40960, 300], P(('genes', 'cols'))
- preservation: float32 [2, 300], replicated
Inputs may be any that keep to these rules, and one draw needn't show every extreme that they name: `labels`: each row holds exactly one 1; every module has 32 or more genes.
All inputs are finite; a program needn't handle non-finite values.
Results may differ from a plain program's by a relative error of at most 0.0031.
Values may be sent and summed in bfloat16 or wider, within the bound.
A program may use at most 128 MiB of HBM per device.

v0:
```python
import math
import jax
import jax.numpy as jnp
from jax import lax
from jax.sharding import PartitionSpec as P

G = 40960


def standardize(expression, resample):
    boot = jnp.take(expression, resample, axis=0)
    centered = boot - jnp.mean(boot, axis=0, keepdims=True)
    total = jnp.sum(centered * centered, axis=0, keepdims=True)
    return (centered * lax.rsqrt(total + 1e-06)).astype(jnp.bfloat16)


def local_sums(connectivity, labels, ref_kim):
    member = labels.astype(jnp.float32)
    kim = jnp.sum(connectivity * member, axis=1)
    rowsum = jnp.sum(connectivity, axis=1)
    stacked = jnp.stack(
        [kim, kim * kim, ref_kim, ref_kim * ref_kim, kim * ref_kim, rowsum, jnp.ones_like(kim)],
        axis=1,
    )
    return jnp.dot(
        member.T, stacked, precision=lax.Precision.HIGHEST, preferred_element_type=jnp.float32
    )


def preserve(sums, total_genes):
    counts = sums[:, 6]
    mean_x = sums[:, 0] / (counts * counts)
    var_x = jnp.maximum(sums[:, 1] / (counts * counts * counts) - mean_x * mean_x, 0.0001)
    mean_y = sums[:, 2] / counts
    var_y = jnp.maximum(sums[:, 3] / counts - mean_y * mean_y, 0.01)
    cross = sums[:, 4] / (counts * counts) - mean_x * mean_y
    between = (sums[:, 5] - sums[:, 0]) / (counts * (total_genes - counts))
    density = (mean_x - between) * jnp.sqrt(counts / var_x)
    linked = cross * jnp.sqrt(counts / (var_x * var_y))
    return jnp.stack([density, linked], axis=0)


def tile_term(row_block, column_block, column_ids, module_count):
    scores = lax.dot_general(
        row_block, column_block, (((0,), (0,)), ((), ())), preferred_element_type=jnp.float32
    )
    squares = scores * scores
    adjacency = (squares * squares * squares).astype(jnp.bfloat16)
    member_block = (
        column_ids[:, None] == jnp.arange(module_count, dtype=jnp.int32)[None, :]
    ).astype(jnp.bfloat16)
    return jnp.dot(adjacency, member_block, preferred_element_type=jnp.float32)


def add_tiles(carried, row_block, piece, every_ids, shard_width, module_count):
    span_width = piece.shape[1]
    column_step = shard_width * math.gcd(span_width // shard_width, 8)
    steps_total = span_width // column_step

    def one_step(step_index, accumulated):
        columns = lax.dynamic_slice_in_dim(piece, step_index * column_step, column_step, 1)
        column_ids = lax.dynamic_slice_in_dim(every_ids, step_index * column_step, column_step, 0)
        return accumulated + tile_term(row_block, columns, column_ids, module_count)

    return lax.fori_loop(0, steps_total, one_step, carried)


def local(expression, resample, labels, ref_kim):
    scaled = standardize(expression, resample)
    module_count = labels.shape[1]
    shard_width = scaled.shape[1]
    module_ids = jnp.sum(labels * jnp.arange(module_count, dtype=jnp.int32)[None, :], axis=1)
    row_block = lax.all_gather(scaled, "cols", axis=1, tiled=True)
    panel_ids = lax.all_gather(module_ids, "genes", axis=0, tiled=True)
    initial = jnp.zeros((row_block.shape[1], module_count), jnp.float32)
    partial_value = add_tiles(
        initial,
        row_block,
        lax.all_gather(scaled, "genes", axis=1, tiled=True),
        panel_ids,
        shard_width,
        module_count,
    )
    connectivity = lax.psum_scatter(partial_value, "cols", scatter_dimension=0, tiled=True)
    sums = lax.psum(local_sums(connectivity, labels, ref_kim), ("genes", "cols"))
    return (connectivity, preserve(sums, G))


def solution(mesh):
    placed = (P(None, ("genes", "cols")), P(), P(("genes", "cols"), None), P(("genes", "cols")))
    return jax.shard_map(
        local,
        mesh=mesh,
        in_specs=placed,
        out_specs=(P(("genes", "cols"), None), P()),
        check_vma=False,
    )
```

profile of v0, /device:TPU:0, one launch (start us, length us, event | category | flops | bytes accessed | tf_op | source)
XLA Modules:
  0.0 391.7 jit_solution(1327400909456358095)
XLA Ops:
  7.2 0.8 compare_select_fusion
  8.0 0.7 compare_and_fusion
  8.8 2.7 gather_fusion
  11.5 1.9 select_reduce_fusion
  14.0 1.3 multiply_convert_fusion
  15.3 0.7 all-gather.4.cloned.1.call-update
  16.3 23.3 %all-gather = s32[16,1,1280]{2,1,0:T(1,128)S(1)} all-gather(s32[1,1,1280]{2,1,0:T(1,128)S(1)} %reshape.229), channel_id=1, replica_groups=mesh['genes'=16,'cols'=2] {'genes'}, dimensions={0}, use_global_device_ids=true | all-gather | bytes 87040 | tf_op jit(solution)/shard_map/all_gather | solution.py:74
  39.6 10.2 %all-gather.6.cloned.1.call-done = bf16[384,2560]{1,0:T(8,128)(2,1)} async-done(((bf16[384,1280]{1,0:T(8,128)(2,1)}), bf16[384,2560]{1,0:T(8,128)(2,1)}) %all-gather.6.cloned.1.call-update) | async-done | bytes 1966096 | tf_op jit(solution)/shard_map/all_gather | solution.py:73
  49.8 122.7 %all-gather.4.cloned.1.call-done = bf16[384,20480]{1,0:T(8,128)(2,1)} async-done(((bf16[384,1280]{1,0:T(8,128)(2,1)}), bf16[384,20480]{1,0:T(8,128)(2,1)}) %all-gather.4.cloned.1.call-update) | async-done | bytes 15728656 | tf_op jit(solution)/shard_map/all_gather | solution.py:79
  172.5 124.2 %while.14 = (s32[]{:T(128)}, f32[2560,300]{0,1:T(8,128)}, bf16[384,20480]{1,0:T(8,128)(2,1)}, bf16[384,2560]{1,0:T(8,128)(2,1)}, s32[20480]{0:T(1024)S(1)}, /*index=5*/s32[]{:T(128)}, s32[]{:T(128)}, s32[]{:T(128)}, s32[]{:T(128)}) while((s32[]{:T(128)}, f32[2560,300]{0,1:T(8,128)}, bf16[384,20480]{1,0:T(8,128)(2,1)}, ...), condition=%wide.region_4.5_spmd.clone, body=%wide.region_3.4_spmd.clone.sunk | while | flops 35970764800 | bytes 120955040 | solution.py:65
  172.5 37.4 %fusion.clone.9 = bf16[2560,10240]{0,1:T(8,128)(2,1)} fusion(bf16[384,2560]{1,0:T(8,128)(2,1)} %get-tuple-element.184, bf16[384,20480]{1,0:T(8,128)(2,1)} %get-tuple-element.183, s32[]{:T(128)S(6)} %select_n.27), kind=kOutput, calls=%fused_computation.2.clone.clone.clone.clone.clone.2.clone.1 | convolution fusion | flops 20237516800 | bytes 62259204 | tf_op jit(solution)/shard_map/while/body/eval_jaxpr/dot_general | solution.py:44
  209.9 24.2 %fusion.47 = f32[2560,300]{0,1:T(8,128)} fusion(s32[10240]{0:T(1024)S(1)} %dynamic_slice.28, f32[2560,300]{0,1:T(8,128)} %get-tuple-element.173, pred[]{:T(512)S(6)} %compare.3, bf16[2560,10240]{0,1:T(8,128)(2,1)} %fusion.clone.9), kind=kOutput, calls=%fused_computation.7.clone.3 | convolution fusion | flops 15733248000 | bytes 58613760 | tf_op jit(solution)/shard_map/while/body/eval_jaxpr/dot_general | solution.py:52
  234.1 37.4 %fusion.clone.9 = bf16[2560,10240]{0,1:T(8,128)(2,1)} fusion(bf16[384,2560]{1,0:T(8,128)(2,1)} %get-tuple-element.184, bf16[384,20480]{1,0:T(8,128)(2,1)} %get-tuple-element.183, s32[]{:T(128)S(6)} %select_n.27), kind=kOutput, calls=%fused_computation.2.clone.clone.clone.clone.clone.2.clone.1 | convolution fusion | flops 20237516800 | bytes 62259204 | tf_op jit(solution)/shard_map/while/body/eval_jaxpr/dot_general | solution.py:44
  271.6 25.1 %fusion.47 = f32[2560,300]{0,1:T(8,128)} fusion(s32[10240]{0:T(1024)S(1)} %dynamic_slice.28, f32[2560,300]{0,1:T(8,128)} %get-tuple-element.173, pred[]{:T(512)S(6)} %compare.3, bf16[2560,10240]{0,1:T(8,128)(2,1)} %fusion.clone.9), kind=kOutput, calls=%fused_computation.7.clone.3 | convolution fusion | flops 15733248000 | bytes 58613760 | tf_op jit(solution)/shard_map/while/body/eval_jaxpr/dot_general | solution.py:52
  296.7 0.7 copy-done.5
  297.4 40.6 %reduce-scatter.2.cloned.1.call-done = f32[1280,300]{0,1:T(8,128)} async-done(((f32[2560,300]{0,1:T(8,128)}), f32[1280,300]{0,1:T(8,128)}) %reduce-scatter.2.cloned.1.call-update) | async-done | bytes 1536016 | tf_op jit(solution)/shard_map/reduce_scatter | solution.py:84
  338.0 1.6 fusion.26
  339.7 0.6 stack.27
  340.3 0.6 stack.28
  340.9 0.6 stack_broadcast_in_dim.3
  341.5 1.4 stack.29
  342.9 2.1 fusion.12
  345.0 39.5 %psum.7 = f32[300,7]{0,1:T(8,128)S(1)} all-reduce(f32[300,7]{0,1:T(8,128)S(1)} %fusion.12), channel_id=1, replica_groups=mesh['genes'=16,'cols'=2] {'genes','cols'}, use_global_device_ids=true, to_apply=%region_8.9 | all-reduce | flops 2100 | bytes 16800 | tf_op jit(solution)/shard_map/psum | solution.py:85
  384.6 0.6 pad_maximum_fusion
  (32 shorter events, 1.0 us)
Async XLA Ops:
  7.2 1.6 copy-start
  7.2 42.6 %all-gather.6.cloned.1.call-start = ((), (), s32[]{:S(2)}) async-start(), calls=%async_computation.2 | async-start | bytes 2949120 | tf_op jit(solution)/shard_map/all_gather | solution.py:73
  11.5 2.1 copy-start.2
  14.0 2.1 copy-start.3
  15.3 157.2 %all-gather.4.cloned.1.call-start = ((), (), s32[]{:S(2)}) async-start(), calls=%async_computation.1 | async-start | bytes 16711680 | tf_op jit(solution)/shard_map/all_gather | solution.py:79
  16.0 322.0 %reduce-scatter.2.cloned.1.call-start = ((), (), s32[]{:S(2)}) async-start(), calls=%async_computation.3 | async-start | bytes 4669440 | tf_op jit(solution)/shard_map/reduce_scatter | solution.py:84
  296.7 0.7 copy-start.5
  296.7 41.4 %copy-start.4 = (s32[1280,300]{0,1:T(8,128)S(1)}, s32[1280,300]{0,1:T(8,128)}, u32[]{:S(2)}) copy-start(s32[1280,300]{0,1:T(8,128)} %param.8) | copy-start | bytes 4608004
  297.4 87.8 %copy-start.1 = (f32[384,1280]{1,0:T(8,128)S(1)}, f32[384,1280]{1,0:T(8,128)}, u32[]{:S(2)}) copy-start(f32[384,1280]{1,0:T(8,128)} %param.6) | copy-start | bytes 5898244
Sparse Core Ops, SparseCore 0:
  15.4 34.3 all-gather.5
  52.6 119.7 all-gather.3
  296.8 41.1 reduce-scatter.1
where the time goes:
time: 392 us
  waiting for transfers between devices  174 us (44%)
  matrix products  126 us (32%)
  blocking collectives  62.8 us (16%)
  between operations  13.9 us (4%)
  other arithmetic  7.47 us (2%)
  local copies, waits for them, and re-layouts  6.83 us (2%)
    all_gather x1, waiting for transfers between devices, local(): lax.all_gather(scaled, 'genes', axis=1, tiled=True)  123 us
    dot_general x2, matrix products, tile_term(): lax.dot_general(row_block, column_block, (((0,), (0,)), ((), ())), prefer...  74.9 us
    dot_general x2, matrix products, tile_term(): return jnp.dot(adjacency, member_block, preferred_element_type=jnp.float32)  49.3 us
    reduce_scatter x1, waiting for transfers between devices, local(): lax.psum_scatter(partial_value, 'cols', scatter_dimension=0, tiled=True)  40.6 us
    psum x1, blocking collectives, local(): lax.psum(local_sums(connectivity, labels, ref_kim), ('genes', 'cols'))  39.5 us
    all_gather x1, blocking collectives, local(): panel_ids = lax.all_gather(module_ids, 'genes', axis=0, tiled=True)  23.3 us
    all_gather x1, waiting for transfers between devices, local(): row_block = lax.all_gather(scaled, 'cols', axis=1, tiled=True)  10.2 us
  transfers between devices with their start and end apart: 3, of which 3 were waited for; matrix products, arithmetic and copies ran while one was open for 0% of the time, Pallas kernels for 0%

commit v1 on v0

--- a/solution.py
+++ b/solution.py
@@ -71,7 +71,13 @@
     shard_width = scaled.shape[1]
     module_ids = jnp.sum(labels * jnp.arange(module_count, dtype=jnp.int32)[None, :], axis=1)
     row_block = lax.all_gather(scaled, "cols", axis=1, tiled=True)
-    panel_ids = lax.all_gather(module_ids, "genes", axis=0, tiled=True)
+    count = lax.axis_size("genes")
+    moving, shards = (module_ids, [module_ids])
+    for _ in range(count - 1):
+        moving = lax.ppermute(moving, "genes", [(i, (i + 1) % count) for i in range(count)])
+        shards.insert(0, moving)
+    row_of_blocks = jnp.concatenate(shards, axis=0)
+    panel_ids = jnp.roll(row_of_blocks, (lax.axis_index("genes") + 1) * module_ids.shape[0], axis=0)
     initial = jnp.zeros((row_block.shape[1], module_count), jnp.float32)
     partial_value = add_tiles(
         initial,

time: 392 us -> 393 us (level)
  blocking collectives: 62.8 us -> 39.4 us
  waiting for transfers between devices: 174 us -> 197 us
    ppermute x0 -> x15, waiting for transfers between devices: none -> 89 us  [local(): lax.ppermute(moving, 'genes', [(i, (i + 1) % count) for i in range(count)])]
    all_gather x1, waiting for transfers between devices: 123 us -> 66.5 us  [local(): lax.all_gather(scaled, 'genes', axis=1, tiled=True)]
    all_gather x1 -> x0, blocking collectives: 23.3 us -> none  [local(): panel_ids = lax.all_gather(module_ids, 'genes', axis=0, tiled=True)]
    all_gather x1, waiting for transfers between devices: 10.2 us -> 0.02 us  [local(): row_block = lax.all_gather(scaled, 'cols', axis=1, tiled=True)]
  transfers between devices with their start and end apart: 3 -> 18, of which waited for: 3 -> 17; matrix products, arithmetic and copies ran while one was open for 0% -> 0% of each run, Pallas kernels for 0% -> 0%
where the time goes in v1:
time: 393 us; the launch traced here: 392 us
  waiting for transfers between devices  197 us (50%)
  matrix products  126 us (32%)
  blocking collectives  39.4 us (10%)
  between operations  14.1 us (4%)
  other arithmetic  7.47 us (2%)
  local copies, waits for them, and re-layouts  7.12 us (2%)
    ppermute x15, waiting for transfers between devices, local(): lax.ppermute(moving, 'genes', [(i, (i + 1) % count) for i in range(count)])  89 us
    dot_general x2, matrix products, tile_term(): lax.dot_general(row_block, column_block, (((0,), (0,)), ((), ())), prefer...  74.9 us
    all_gather x1, waiting for transfers between devices, local(): lax.all_gather(scaled, 'genes', axis=1, tiled=True)  66.5 us
    dot_general x2, matrix products, tile_term(): return jnp.dot(adjacency, member_block, preferred_element_type=jnp.float32)  49.4 us
    reduce_scatter x1, waiting for transfers between devices, local(): lax.psum_scatter(partial_value, 'cols', scatter_dimension=0, tiled=True)  40.7 us
    psum x1, blocking collectives, local(): lax.psum(local_sums(connectivity, labels, ref_kim), ('genes', 'cols'))  39.4 us
  transfers between devices with their start and end apart: 18, of which 17 were waited for; matrix products, arithmetic and copies ran while one was open for 0% of the time, Pallas kernels for 0%

profile of v1, /device:TPU:0, one launch (start us, length us, event | category | flops | bytes accessed | tf_op | source)
XLA Modules:
  0.0 392.2 jit_solution(15066444766066820533)
XLA Ops:
  8.8 2.7 gather_fusion
  16.8 6.3 %collective-permute-done = s32[1280]{0:T(1024)S(1)} collective-permute-done((s32[1280]{0:T(1024)S(1)}, s32[1280]{0:T(1024)S(1)}, u32[]{:S(2)}, u32[]{:S(2)}) %collective-permute-start) | collective-permute-done | bytes 5152 | tf_op jit(solution)/shard_map/ppermute | solution.py:77
  23.1 5.8 %collective-permute-done.1 = s32[1280]{0:T(1024)S(1)} collective-permute-done((s32[1280]{0:T(1024)S(1)}, s32[1280]{0:T(1024)S(1)}, u32[]{:S(2)}, u32[]{:S(2)}) %collective-permute-start.1) | collective-permute-done | bytes 5152 | tf_op jit(solution)/shard_map/ppermute | solution.py:77
  28.8 5.8 %collective-permute-done.2 = s32[1280]{0:T(1024)S(1)} collective-permute-done((s32[1280]{0:T(1024)S(1)}, s32[1280]{0:T(1024)S(1)}, u32[]{:S(2)}, u32[]{:S(2)}) %collective-permute-start.2) | collective-permute-done | bytes 5152 | tf_op jit(solution)/shard_map/ppermute | solution.py:77
  34.6 5.8 %collective-permute-done.3 = s32[1280]{0:T(1024)S(1)} collective-permute-done((s32[1280]{0:T(1024)S(1)}, s32[1280]{0:T(1024)S(1)}, u32[]{:S(2)}, u32[]{:S(2)}) %collective-permute-start.3) | collective-permute-done | bytes 5152 | tf_op jit(solution)/shard_map/ppermute | solution.py:77
  40.4 5.8 %collective-permute-done.4 = s32[1280]{0:T(1024)S(1)} collective-permute-done((s32[1280]{0:T(1024)S(1)}, s32[1280]{0:T(1024)S(1)}, u32[]{:S(2)}, u32[]{:S(2)}) %collective-permute-start.4) | collective-permute-done | bytes 5152 | tf_op jit(solution)/shard_map/ppermute | solution.py:77
  46.2 5.8 %collective-permute-done.5 = s32[1280]{0:T(1024)S(1)} collective-permute-done((s32[1280]{0:T(1024)S(1)}, s32[1280]{0:T(1024)S(1)}, u32[]{:S(2)}, u32[]{:S(2)}) %collective-permute-start.5) | collective-permute-done | bytes 5152 | tf_op jit(solution)/shard_map/ppermute | solution.py:77
  51.9 5.8 %collective-permute-done.6 = s32[1280]{0:T(1024)S(1)} collective-permute-done((s32[1280]{0:T(1024)S(1)}, s32[1280]{0:T(1024)S(1)}, u32[]{:S(2)}, u32[]{:S(2)}) %collective-permute-start.6) | collective-permute-done | bytes 5152 | tf_op jit(solution)/shard_map/ppermute | solution.py:77
  57.7 5.8 %collective-permute-done.7 = s32[1280]{0:T(1024)S(1)} collective-permute-done((s32[1280]{0:T(1024)S(1)}, s32[1280]{0:T(1024)S(1)}, u32[]{:S(2)}, u32[]{:S(2)}) %collective-permute-start.7) | collective-permute-done | bytes 5152 | tf_op jit(solution)/shard_map/ppermute | solution.py:77
  63.5 6.2 %collective-permute-done.8 = s32[1280]{0:T(1024)S(1)} collective-permute-done((s32[1280]{0:T(1024)S(1)}, s32[1280]{0:T(1024)S(1)}, u32[]{:S(2)}, u32[]{:S(2)}) %collective-permute-start.8) | collective-permute-done | bytes 5152 | tf_op jit(solution)/shard_map/ppermute | solution.py:77
  69.7 6.1 %collective-permute-done.9 = s32[1280]{0:T(1024)S(1)} collective-permute-done((s32[1280]{0:T(1024)S(1)}, s32[1280]{0:T(1024)S(1)}, u32[]{:S(2)}, u32[]{:S(2)}) %collective-permute-start.9) | collective-permute-done | bytes 5152 | tf_op jit(solution)/shard_map/ppermute | solution.py:77
  75.7 6.2 %collective-permute-done.10 = s32[1280]{0:T(1024)S(1)} collective-permute-done((s32[1280]{0:T(1024)S(1)}, s32[1280]{0:T(1024)S(1)}, u32[]{:S(2)}, u32[]{:S(2)}) %collective-permute-start.10) | collective-permute-done | bytes 5152 | tf_op jit(solution)/shard_map/ppermute | solution.py:77
  81.9 6.1 %collective-permute-done.11 = s32[1280]{0:T(1024)S(1)} collective-permute-done((s32[1280]{0:T(1024)S(1)}, s32[1280]{0:T(1024)S(1)}, u32[]{:S(2)}, u32[]{:S(2)}) %collective-permute-start.11) | collective-permute-done | bytes 5152 | tf_op jit(solution)/shard_map/ppermute | solution.py:77
  88.0 6.2 %collective-permute-done.12 = s32[1280]{0:T(1024)S(1)} collective-permute-done((s32[1280]{0:T(1024)S(1)}, s32[1280]{0:T(1024)S(1)}, u32[]{:S(2)}, u32[]{:S(2)}) %collective-permute-start.12) | collective-permute-done | bytes 5152 | tf_op jit(solution)/shard_map/ppermute | solution.py:77
  94.2 5.8 %collective-permute-done.13 = s32[1280]{0:T(1024)S(1)} collective-permute-done((s32[1280]{0:T(1024)S(1)}, s32[1280]{0:T(1024)S(1)}, u32[]{:S(2)}, u32[]{:S(2)}) %collective-permute-start.13) | collective-permute-done | bytes 5152 | tf_op jit(solution)/shard_map/ppermute | solution.py:77
  99.9 5.9 %collective-permute-done.14 = s32[1280]{0:T(1024)S(1)} collective-permute-done((s32[1280]{0:T(1024)S(1)}, s32[1280]{0:T(1024)S(1)}, u32[]{:S(2)}, u32[]{:S(2)}) %collective-permute-start.14) | collective-permute-done | bytes 5152 | tf_op jit(solution)/shard_map/ppermute | solution.py:77
  106.4 66.5 %all-gather.3.cloned.1.call-done = bf16[384,20480]{1,0:T(8,128)(2,1)} async-done(((bf16[384,1280]{1,0:T(8,128)(2,1)}), bf16[384,20480]{1,0:T(8,128)(2,1)}) %all-gather.3.cloned.1.call-update) | async-done | bytes 15728656 | tf_op jit(solution)/shard_map/all_gather | solution.py:85
  172.9 124.3 %while.14 = (s32[]{:T(128)}, f32[2560,300]{0,1:T(8,128)}, bf16[384,20480]{1,0:T(8,128)(2,1)}, bf16[384,2560]{1,0:T(8,128)(2,1)}, s32[20480]{0:T(1024)S(1)}, /*index=5*/s32[]{:T(128)}, s32[]{:T(128)}, s32[]{:T(128)}, s32[]{:T(128)}) while((s32[]{:T(128)}, f32[2560,300]{0,1:T(8,128)}, bf16[384,20480]{1,0:T(8,128)(2,1)}, ...), condition=%wide.region_4.5_spmd.clone, body=%wide.region_3.4_spmd.clone.sunk | while | flops 35970764800 | bytes 120955040 | solution.py:65
  172.9 37.4 %fusion.clone.9 = bf16[2560,10240]{0,1:T(8,128)(2,1)} fusion(bf16[384,2560]{1,0:T(8,128)(2,1)} %get-tuple-element.184, bf16[384,20480]{1,0:T(8,128)(2,1)} %get-tuple-element.183, s32[]{:T(128)S(6)} %select_n.42), kind=kOutput, calls=%fused_computation.2.clone.clone.clone.clone.clone.2.clone.1 | convolution fusion | flops 20237516800 | bytes 62259204 | tf_op jit(solution)/shard_map/while/body/eval_jaxpr/dot_general | solution.py:44
  210.4 24.2 %fusion.47 = f32[2560,300]{0,1:T(8,128)} fusion(s32[10240]{0:T(1024)S(1)} %dynamic_slice.33, f32[2560,300]{0,1:T(8,128)} %get-tuple-element.173, pred[]{:T(512)S(6)} %compare.3, bf16[2560,10240]{0,1:T(8,128)(2,1)} %fusion.clone.9), kind=kOutput, calls=%fused_computation.7.clone.3 | convolution fusion | flops 15733248000 | bytes 58613760 | tf_op jit(solution)/shard_map/while/body/eval_jaxpr/dot_general | solution.py:52
  234.6 37.4 %fusion.clone.9 = bf16[2560,10240]{0,1:T(8,128)(2,1)} fusion(bf16[384,2560]{1,0:T(8,128)(2,1)} %get-tuple-element.184, bf16[384,20480]{1,0:T(8,128)(2,1)} %get-tuple-element.183, s32[]{:T(128)S(6)} %select_n.42), kind=kOutput, calls=%fused_computation.2.clone.clone.clone.clone.clone.2.clone.1 | convolution fusion | flops 20237516800 | bytes 62259204 | tf_op jit(solution)/shard_map/while/body/eval_jaxpr/dot_general | solution.py:44
  272.0 25.1 %fusion.47 = f32[2560,300]{0,1:T(8,128)} fusion(s32[10240]{0:T(1024)S(1)} %dynamic_slice.33, f32[2560,300]{0,1:T(8,128)} %get-tuple-element.173, pred[]{:T(512)S(6)} %compare.3, bf16[2560,10240]{0,1:T(8,128)(2,1)} %fusion.clone.9), kind=kOutput, calls=%fused_computation.7.clone.3 | convolution fusion | flops 15733248000 | bytes 58613760 | tf_op jit(solution)/shard_map/while/body/eval_jaxpr/dot_general | solution.py:52
  297.9 40.7 %reduce-scatter.2.cloned.1.call-done = f32[1280,300]{0,1:T(8,128)} async-done(((f32[2560,300]{0,1:T(8,128)}), f32[1280,300]{0,1:T(8,128)}) %reduce-scatter.2.cloned.1.call-update) | async-done | bytes 1536016 | tf_op jit(solution)/shard_map/reduce_scatter | solution.py:90
  345.6 39.4 %psum.7 = f32[300,7]{0,1:T(8,128)S(1)} all-reduce(f32[300,7]{0,1:T(8,128)S(1)} %fusion.12), channel_id=1, replica_groups=mesh['genes'=16,'cols'=2] {'genes','cols'}, use_global_device_ids=true, to_apply=%region_8.9 | all-reduce | flops 2100 | bytes 16800 | tf_op jit(solution)/shard_map/psum | solution.py:91
  (94 shorter events, 15.4 us)
Async XLA Ops:
  7.2 1.6 copy-start
  7.2 99.2 %all-gather.5.cloned.1.call-start = ((), (), s32[]{:S(2)}) async-start(), calls=%async_computation.2 | async-start | bytes 2949120 | tf_op jit(solution)/shard_map/all_gather | solution.py:73
  11.4 2.1 copy-start.2
  13.9 2.1 copy-start.3
  15.2 157.7 %all-gather.3.cloned.1.call-start = ((), (), s32[]{:S(2)}) async-start(), calls=%async_computation.1 | async-start | bytes 16711680 | tf_op jit(solution)/shard_map/all_gather | solution.py:85
  16.0 322.6 %reduce-scatter.2.cloned.1.call-start = ((), (), s32[]{:S(2)}) async-start(), calls=%async_computation.3 | async-start | bytes 4669440 | tf_op jit(solution)/shard_map/reduce_scatter | solution.py:90
  16.2 6.9 %collective-permute-start = (s32[1280]{0:T(1024)S(1)}, s32[1280]{0:T(1024)S(1)}, u32[]{:S(2)}, u32[]{:S(2)}) collective-permute-start(s32[1280]{0:T(1024)S(1)} %multiply_reduce_fusion.2), channel_id=1, source_target_pairs={{0,2},{2,4},{4,6},{6,8},{8,10},{10,12},{12,14},{14,16},{16,18},{18... | collective-permute-start | bytes 15368 | tf_op jit(solution)/shard_map/ppermute | solution.py:77
  23.1 5.8 %collective-permute-start.1 = (s32[1280]{0:T(1024)S(1)}, s32[1280]{0:T(1024)S(1)}, u32[]{:S(2)}, u32[]{:S(2)}) collective-permute-start(s32[1280]{0:T(1024)S(1)} %collective-permute-done), channel_id=1, source_target_pairs={{0,2},{2,4},{4,6},{6,8},{8,10},{10,12},{12,14},{14,16},{16,18},{18... | collective-permute-start | bytes 15368 | tf_op jit(solution)/shard_map/ppermute | solution.py:77
  28.8 5.8 %collective-permute-start.2 = (s32[1280]{0:T(1024)S(1)}, s32[1280]{0:T(1024)S(1)}, u32[]{:S(2)}, u32[]{:S(2)}) collective-permute-start(s32[1280]{0:T(1024)S(1)} %collective-permute-done.1), channel_id=1, source_target_pairs={{0,2},{2,4},{4,6},{6,8},{8,10},{10,12},{12,14},{14,16},{16,18},{18... | collective-permute-start | bytes 15368 | tf_op jit(solution)/shard_map/ppermute | solution.py:77
  34.6 5.8 %collective-permute-start.3 = (s32[1280]{0:T(1024)S(1)}, s32[1280]{0:T(1024)S(1)}, u32[]{:S(2)}, u32[]{:S(2)}) collective-permute-start(s32[1280]{0:T(1024)S(1)} %collective-permute-done.2), channel_id=1, source_target_pairs={{0,2},{2,4},{4,6},{6,8},{8,10},{10,12},{12,14},{14,16},{16,18},{18... | collective-permute-start | bytes 15368 | tf_op jit(solution)/shard_map/ppermute | solution.py:77
  40.4 5.8 %collective-permute-start.4 = (s32[1280]{0:T(1024)S(1)}, s32[1280]{0:T(1024)S(1)}, u32[]{:S(2)}, u32[]{:S(2)}) collective-permute-start(s32[1280]{0:T(1024)S(1)} %collective-permute-done.3), channel_id=1, source_target_pairs={{0,2},{2,4},{4,6},{6,8},{8,10},{10,12},{12,14},{14,16},{16,18},{18... | collective-permute-start | bytes 15368 | tf_op jit(solution)/shard_map/ppermute | solution.py:77
  46.2 5.8 %collective-permute-start.5 = (s32[1280]{0:T(1024)S(1)}, s32[1280]{0:T(1024)S(1)}, u32[]{:S(2)}, u32[]{:S(2)}) collective-permute-start(s32[1280]{0:T(1024)S(1)} %collective-permute-done.4), channel_id=1, source_target_pairs={{0,2},{2,4},{4,6},{6,8},{8,10},{10,12},{12,14},{14,16},{16,18},{18... | collective-permute-start | bytes 15368 | tf_op jit(solution)/shard_map/ppermute | solution.py:77
  51.9 5.8 %collective-permute-start.6 = (s32[1280]{0:T(1024)S(1)}, s32[1280]{0:T(1024)S(1)}, u32[]{:S(2)}, u32[]{:S(2)}) collective-permute-start(s32[1280]{0:T(1024)S(1)} %collective-permute-done.5), channel_id=1, source_target_pairs={{0,2},{2,4},{4,6},{6,8},{8,10},{10,12},{12,14},{14,16},{16,18},{18... | collective-permute-start | bytes 15368 | tf_op jit(solution)/shard_map/ppermute | solution.py:77
  57.7 5.8 %collective-permute-start.7 = (s32[1280]{0:T(1024)S(1)}, s32[1280]{0:T(1024)S(1)}, u32[]{:S(2)}, u32[]{:S(2)}) collective-permute-start(s32[1280]{0:T(1024)S(1)} %collective-permute-done.6), channel_id=1, source_target_pairs={{0,2},{2,4},{4,6},{6,8},{8,10},{10,12},{12,14},{14,16},{16,18},{18... | collective-permute-start | bytes 15368 | tf_op jit(solution)/shard_map/ppermute | solution.py:77
  63.5 6.2 %collective-permute-start.8 = (s32[1280]{0:T(1024)S(1)}, s32[1280]{0:T(1024)S(1)}, u32[]{:S(2)}, u32[]{:S(2)}) collective-permute-start(s32[1280]{0:T(1024)S(1)} %collective-permute-done.7), channel_id=1, source_target_pairs={{0,2},{2,4},{4,6},{6,8},{8,10},{10,12},{12,14},{14,16},{16,18},{18... | collective-permute-start | bytes 15368 | tf_op jit(solution)/shard_map/ppermute | solution.py:77
  69.7 6.1 %collective-permute-start.9 = (s32[1280]{0:T(1024)S(1)}, s32[1280]{0:T(1024)S(1)}, u32[]{:S(2)}, u32[]{:S(2)}) collective-permute-start(s32[1280]{0:T(1024)S(1)} %collective-permute-done.8), channel_id=1, source_target_pairs={{0,2},{2,4},{4,6},{6,8},{8,10},{10,12},{12,14},{14,16},{16,18},{18... | collective-permute-start | bytes 15368 | tf_op jit(solution)/shard_map/ppermute | solution.py:77
  75.7 6.2 %collective-permute-start.10 = (s32[1280]{0:T(1024)S(1)}, s32[1280]{0:T(1024)S(1)}, u32[]{:S(2)}, u32[]{:S(2)}) collective-permute-start(s32[1280]{0:T(1024)S(1)} %collective-permute-done.9), channel_id=1, source_target_pairs={{0,2},{2,4},{4,6},{6,8},{8,10},{10,12},{12,14},{14,16},{16,18},{18... | collective-permute-start | bytes 15368 | tf_op jit(solution)/shard_map/ppermute | solution.py:77
  81.9 6.1 %collective-permute-start.11 = (s32[1280]{0:T(1024)S(1)}, s32[1280]{0:T(1024)S(1)}, u32[]{:S(2)}, u32[]{:S(2)}) collective-permute-start(s32[1280]{0:T(1024)S(1)} %collective-permute-done.10), channel_id=1, source_target_pairs={{0,2},{2,4},{4,6},{6,8},{8,10},{10,12},{12,14},{14,16},{16,18},{18... | collective-permute-start | bytes 15368 | tf_op jit(solution)/shard_map/ppermute | solution.py:77
  88.0 6.2 %collective-permute-start.12 = (s32[1280]{0:T(1024)S(1)}, s32[1280]{0:T(1024)S(1)}, u32[]{:S(2)}, u32[]{:S(2)}) collective-permute-start(s32[1280]{0:T(1024)S(1)} %collective-permute-done.11), channel_id=1, source_target_pairs={{0,2},{2,4},{4,6},{6,8},{8,10},{10,12},{12,14},{14,16},{16,18},{18... | collective-permute-start | bytes 15368 | tf_op jit(solution)/shard_map/ppermute | solution.py:77
  94.2 5.8 %collective-permute-start.13 = (s32[1280]{0:T(1024)S(1)}, s32[1280]{0:T(1024)S(1)}, u32[]{:S(2)}, u32[]{:S(2)}) collective-permute-start(s32[1280]{0:T(1024)S(1)} %collective-permute-done.12), channel_id=1, source_target_pairs={{0,2},{2,4},{4,6},{6,8},{8,10},{10,12},{12,14},{14,16},{16,18},{18... | collective-permute-start | bytes 15368 | tf_op jit(solution)/shard_map/ppermute | solution.py:77
  99.9 5.9 %collective-permute-start.14 = (s32[1280]{0:T(1024)S(1)}, s32[1280]{0:T(1024)S(1)}, u32[]{:S(2)}, u32[]{:S(2)}) collective-permute-start(s32[1280]{0:T(1024)S(1)} %collective-permute-done.13), channel_id=1, source_target_pairs={{0,2},{2,4},{4,6},{6,8},{8,10},{10,12},{12,14},{14,16},{16,18},{18... | collective-permute-start | bytes 15368 | tf_op jit(solution)/shard_map/ppermute | solution.py:77
  297.2 0.7 copy-start.5
  297.2 41.4 %copy-start.4 = (s32[1280,300]{0,1:T(8,128)S(1)}, s32[1280,300]{0,1:T(8,128)}, u32[]{:S(2)}) copy-start(s32[1280,300]{0,1:T(8,128)} %param.8) | copy-start | bytes 4608004
  297.9 87.8 %copy-start.1 = (f32[384,1280]{1,0:T(8,128)S(1)}, f32[384,1280]{1,0:T(8,128)}, u32[]{:S(2)}) copy-start(f32[384,1280]{1,0:T(8,128)} %param.6) | copy-start | bytes 5898244
Sparse Core Ops, SparseCore 0:
  15.4 34.3 all-gather.4
  52.6 120.2 all-gather.2
  297.3 41.1 reduce-scatter.1
